TPU v7x, 32 devices: a whole 2x2x4 slice. The times are simulated.
32 devices in a mesh: batch: 4 (over z), row: 4 (over x, core), col: 2 (over y).
Axes of the slice: x: 2, y: 2, z: 4, core: 2. Of those that a mesh axis runs over, the one named last changes fastest.
Arguments:
- embeddings: bfloat16 [512, 128, 512], P('batch', 'col', 'row'), may hold values from -170 to 170
- projection: bfloat16 [512, 32], replicated, may hold values from -0.25 to 0.25
- w_in: bfloat16 [16384, 2048], P('row', 'col'), may hold values from -0.046875 to 0.046875
- bias: float32 [2048], P('col'), may hold values from -3 to 3
- w_out: bfloat16 [2048, 128, 512], P(None, 'col', 'row'), may hold values from -0.125 to 0.125
- cotangent: bfloat16 [512, 128, 512], P('batch', 'col', 'row'), may hold values from -0.1796875 to 0.1796875
Outputs:
- mixed: bfloat16 [512, 128, 512], P('batch', 'col', 'row')
- grad_out: float32 [2048, 128, 512], P('batch', 'col', 'row')
- grad_in: float32 [16384, 2048], P('row', 'col')
- grad_bias: float32 [2048], P('col')
- grad_proj: float32 [512, 32], P('row')
All inputs are finite; a program needn't handle non-finite values.
Results may differ from a plain program's by a relative error of at most 0.006.
Values may be sent and summed in bfloat16 or wider, within the bound.
No kernel may reach another device: no remote copies, remote signals or barrier semaphores. Data moves between devices by JAX's collectives and lax.ppermute only.
A program may use at most 192 MiB of HBM per device.

v0:
```python
import jax
import jax.numpy as jnp
from jax import lax
from jax.sharding import PartitionSpec as P

epsilon = 1e-06


def contract_first(left, right):
    return lax.dot_general(
        left, right, (((0,), (0,)), ((), ())), preferred_element_type=jnp.float32
    )


def contract_last(left, right):
    return lax.dot_general(
        left, right, (((1,), (1,)), ((), ())), preferred_element_type=jnp.float32
    )


def local(embeddings, projection, w_in, bias, w_out, cotangent):
    highest = lax.Precision.HIGHEST
    tok_rows, feat_local, emb_local = embeddings.shape
    rank_cols = projection.shape[1]
    row_count = lax.axis_size("row")
    col_count = lax.axis_size("col")
    col_place = lax.axis_index("col")
    emb_float = embeddings.astype(jnp.float32)
    full_rows = lax.all_gather(embeddings, "col", axis=1, tiled=True)
    regrouped = lax.all_to_all(embeddings, "col", split_axis=2, concat_axis=1, tiled=True)
    column_rows = lax.all_gather(regrouped, "row", axis=2, tiled=True)
    tile_gram = jnp.einsum(
        "bdj,bde->bje", column_rows, full_rows, preferred_element_type=jnp.float32
    )
    block_size = emb_local // col_count
    stacked = projection.reshape(row_count, emb_local, rank_cols)
    chosen = lax.dynamic_slice_in_dim(stacked, col_place * block_size, block_size, 1)
    chosen = chosen.reshape(row_count * block_size, rank_cols).astype(jnp.float32)
    partial_value = jnp.einsum("bje,jk->bek", tile_gram, chosen, precision=highest)
    interact = lax.psum(partial_value, "col")
    feature_count = emb_local * row_count * rank_cols
    square_sum = lax.psum(jnp.sum(interact * interact, axis=(1, 2)), "row")
    inv_rms = lax.rsqrt(square_sum / feature_count + epsilon)[:, None, None]
    normed = interact * inv_rms
    activated = normed.astype(jnp.bfloat16).reshape(tok_rows, emb_local * rank_cols)
    preact = lax.psum(jnp.dot(activated, w_in, preferred_element_type=jnp.float32), "row") + bias
    hidden = jax.nn.silu(preact).astype(jnp.bfloat16)
    hidden_all = lax.all_gather(hidden, "col", axis=1, tiled=True)
    flat_out = w_out.reshape(w_out.shape[0], feat_local * emb_local)
    mixed = (
        jnp.dot(hidden_all, flat_out, preferred_element_type=jnp.float32)
        .astype(jnp.bfloat16)
        .reshape(tok_rows, feat_local, emb_local)
    )
    cot_rows = cotangent.reshape(tok_rows, feat_local * emb_local)
    d_cols = lax.psum_scatter(
        contract_last(cot_rows, flat_out), "col", scatter_dimension=1, tiled=True
    )
    d_hidden = lax.psum(d_cols, "row")
    sigmoid_pre = jax.nn.sigmoid(preact)
    d_preact = d_hidden * sigmoid_pre * (1.0 + preact * (1.0 - sigmoid_pre))
    d_pre_b = d_preact.astype(jnp.bfloat16)
    per_batch = w_out.shape[0] // lax.axis_size("batch")
    every_hidden, every_cot = (
        lax.all_gather(hidden_all, "batch", axis=0, tiled=True),
        lax.all_gather(cot_rows, "batch", axis=0, tiled=True),
    )
    own_hidden = lax.dynamic_slice_in_dim(
        every_hidden, lax.axis_index("batch") * per_batch, per_batch, 1
    )
    grad_flat = contract_first(own_hidden, every_cot)
    grad_out = grad_flat.reshape(per_batch, feat_local, emb_local)
    grad_in, grad_bias = lax.psum(
        (contract_first(activated, d_pre_b), jnp.sum(d_preact, axis=0)), "batch"
    )
    d_act = lax.psum(contract_last(d_pre_b, w_in), "col").reshape(tok_rows, emb_local, rank_cols)
    inner_term = lax.psum(jnp.sum(d_act * normed, axis=(1, 2)), "row") / feature_count
    d_inter = (inv_rms * (d_act - normed * inner_term[:, None, None])).astype(jnp.bfloat16)
    back_fold = lax.psum(
        jnp.einsum("bek,bde->bdk", d_inter, embeddings, preferred_element_type=jnp.float32), "row"
    )
    grad_proj = lax.psum(
        jnp.einsum("bde,bdk->ek", emb_float, back_fold, precision=highest), ("batch", "col")
    )
    return (mixed, grad_out, grad_in, grad_bias, grad_proj)


def solution(mesh):
    placed = (
        P("batch", "col", "row"),
        P(),
        P("row", "col"),
        P("col"),
        P(None, "col", "row"),
        P("batch", "col", "row"),
    )
    return jax.shard_map(
        local,
        mesh=mesh,
        in_specs=placed,
        out_specs=(
            P("batch", "col", "row"),
            P("batch", "col", "row"),
            P("row", "col"),
            P("col"),
            P("row", None),
        ),
        check_vma=False,
    )
```

profile of v0, /device:TPU:0, one launch (start us, length us, event | category | flops | bytes accessed | tf_op | source)
XLA Modules:
  0.0 1151.0 jit_solution(1242558977459168627)
XLA Ops:
  12.9 49.2 %all_to_all.18 = bf16[128,64,128]{0,1,2:T(8,128)(2,1)S(1)} all-to-all(bf16[128,64,128]{0,1,2:T(8,128)(2,1)} %copy.22), channel_id=1, replica_groups=mesh['batch'=4,'row'=4,'col'=2] {'col'}, dimensions={2} | all-to-all | bytes 4194304 | tf_op jit(solution)/shard_map/all_to_all | solution.py:30
  67.7 20.5 %all-gather.7.cloned.1.call-done = bf16[128,128,128]{2,1,0:T(8,128)(2,1)} async-done(((bf16[128,64,128]{2,1,0:T(8,128)(2,1)}), bf16[128,128,128]{2,1,0:T(8,128)(2,1)}) %all-gather.7.cloned.1.call-update) | async-done | bytes 4194320 | tf_op jit(solution)/shard_map/all_gather | solution.py:29
  88.2 60.9 %all-gather.5.cloned.1.call-done = bf16[128,128,256]{1,2,0:T(8,128)(2,1)} async-done(((bf16[128,128,64]{1,2,0:T(8,128)(2,1)}), bf16[128,128,256]{1,2,0:T(8,128)(2,1)}) %all-gather.5.cloned.1.call-update) | async-done | bytes 8388624 | tf_op jit(solution)/shard_map/all_gather | solution.py:31
  149.1 13.1 %fusion.24 = f32[128,256,128]{2,1,0:T(8,128)} fusion(bf16[128,128,256]{1,2,0:T(8,128)(2,1)} %all-gather.5.cloned.1.call-done, bf16[128,128,128]{2,1,0:T(8,128)(2,1)} %all-gather.7.cloned.1.call-done), kind=kOutput, calls=%fused_computation.32 | convolution fusion | flops 1073741824 | bytes 29360128 | tf_op jit(solution)/shard_map/bdj,bde->bje/dot_general | solution.py:32
  162.2 11.5 %fusion.25 = f32[128,128,32]{1,2,0:T(8,128)} fusion(f32[128,256,128]{2,1,0:T(8,128)} %fusion.24, bf16[256,32,1]{0,1,2:T(8,128)(2,1)S(1)} %reshape.45), kind=kOutput, calls=%fused_computation.33 | convolution fusion | flops 1610612736 | bytes 18890752 | tf_op jit(solution)/shard_map/bje,jk->bek/dot_general | solution.py:39
  175.3 21.4 %fusion.8 = f32[128,2048]{1,0:T(8,128)} fusion(bf16[2048,64,128]{2,1,0:T(8,128)(2,1)} %param.10, bf16[128,64,128]{2,1,0:T(8,128)(2,1)S(1)} %copy-done.3), kind=kOutput, calls=%fused_computation.7 | convolution fusion | flops 4294967296 | bytes 36700160 | tf_op jit(solution)/shard_map/dot_general | solution.py:16
  196.8 40.1 %all-reduce.7.cloned.1.call-done = f32[128,128,32]{1,2,0:T(8,128)} async-done(((f32[128,128,32]{1,2,0:T(8,128)}), f32[128,128,32]{1,2,0:T(8,128)}) %all-reduce.7.cloned.1.call-update) | async-done | bytes 2097168 | tf_op jit(solution)/shard_map/psum | solution.py:40
  239.7 6.8 psum.71
  250.2 5.5 fusion.26
  260.0 39.2 %all-reduce.15.cloned.1.call-done = (f32[128,1024]{1,0:T(8,128)}, f32[128,1024]{1,0:T(8,128)}) async-done(((f32[128,1024]{1,0:T(8,128)}, f32[128,1024]{1,0:T(8,128)}), (f32[128,1024]{1,0:T(8,128)}, f32[128,1024]{1,0:T(8,128)})) %all-reduce.15.cloned.1.call-update) | async-done | bytes 1048592 | tf_op jit(solution)/shard_map/psum | solution.py:46
  301.4 7.0 fusion.18
  311.8 63.5 %all-reduce.11.cloned.1.call-done = f32[128,128,32]{1,2,0:T(8,128)} async-done(((f32[128,128,32]{1,2,0:T(8,128)}), f32[128,128,32]{1,2,0:T(8,128)}) %all-reduce.11.cloned.1.call-update) | async-done | bytes 2097168 | tf_op jit(solution)/shard_map/psum | solution.py:76
  378.8 6.4 psum.77
  395.8 8.1 all_gather.17
  404.1 8.5 fusion.20
  413.6 26.8 %fusion.12 = bf16[16,8,64,128]{3,1,2,0:T(8,128)(2,1)} fusion(bf16[128,2048]{1,0:T(8,128)(2,1)S(1)} %copy-done.5, bf16[256,8,64,128]{3,2,1,0:T(8,128)(2,1)} %bitcast.60), kind=kOutput, calls=%fused_computation.14 | convolution fusion | flops 4296015872 | bytes 36175872 | tf_op jit(solution)/shard_map/dot_general | solution.py:51
  444.1 13.1 %psum.75 = f32[1024]{0:T(1024)} all-reduce(f32[1024]{0:T(1024)S(1)} %get-tuple-element.7), channel_id=1, replica_groups=mesh['batch'=4,'row'=4,'col'=2] {'batch'}, use_global_device_ids=true, to_apply=%region_8.9 | all-reduce | flops 1024 | bytes 8192 | tf_op jit(solution)/shard_map/psum | solution.py:73
  459.9 40.4 %psum.79 = f32[128,32]{0,1:T(8,128)} all-reduce(f32[128,32]{0,1:T(8,128)S(1)} %convolution_bitcast_fusion.2), channel_id=1, replica_groups=mesh['batch'=4,'row'=4,'col'=2] {'batch','col'}, use_global_device_ids=true, to_apply=%region_13.14 | all-reduce | flops 4096 | bytes 32768 | tf_op jit(solution)/shard_map/psum | solution.py:82
  500.2 104.9 %all-gather.11.cloned.1.call-done = bf16[512,8192]{1,0:T(8,128)(2,1)} async-done(((bf16[128,8192]{1,0:T(8,128)(2,1)}), bf16[512,8192]{1,0:T(8,128)(2,1)}) %all-gather.11.cloned.1.call-update) | async-done | bytes 8388624 | tf_op jit(solution)/shard_map/all_gather | solution.py:66
  605.2 131.8 %all-gather.9.cloned.1.call-done = bf16[512,2048]{1,0:T(8,128)(2,1)} async-done(((bf16[128,2048]{1,0:T(8,128)(2,1)}), bf16[512,2048]{1,0:T(8,128)(2,1)}) %all-gather.9.cloned.1.call-update) | async-done | bytes 2097168 | tf_op jit(solution)/shard_map/all_gather | solution.py:65
  737.0 7.2 convolution_bitcast_fusion
  744.2 6.9 copy.40
  751.1 380.2 %all-reduce.9.cloned.1.call-done = f32[4096,1024]{1,0:T(8,128)} async-done(((f32[4096,1024]{1,0:T(8,128)}), f32[4096,1024]{1,0:T(8,128)}) %all-reduce.9.cloned.1.call-update) | async-done | bytes 16777232 | tf_op jit(solution)/shard_map/psum | solution.py:73
  1131.4 12.0 %copy.63 = f32[4096,1024]{1,0:T(8,128)} copy(f32[4096,1024]{1,0:T(8,128)} %all-reduce.9.cloned.1.call-done) | data formatting | bytes 33554432
  (58 shorter events, 49.9 us)
Async XLA Ops:
  8.0 1.6 copy-start.1
  8.0 80.2 %all-gather.7.cloned.1.call-start = ((), (), s32[]{:S(2)}) async-start(), calls=%async_computation.3 | async-start | bytes 6291456 | tf_op jit(solution)/shard_map/all_gather | solution.py:29
  8.7 140.4 %all-gather.5.cloned.1.call-start = ((), (), s32[]{:S(2)}) async-start(), calls=%async_computation.2 | async-start | bytes 10485760 | tf_op jit(solution)/shard_map/all_gather | solution.py:31
  66.7 0.8 copy-start.7
  66.8 170.1 %all-reduce.7.cloned.1.call-start = ((), (), s32[]{:S(2)}) async-start(), calls=%async_computation.4 | async-start | bytes 4194304 | tf_op jit(solution)/shard_map/psum | solution.py:40
  173.7 1.6 copy-start.3
  173.7 86.2 %reduce-scatter.2.cloned.1.call-start = ((), (), s32[]{:S(2)}) async-start(), calls=%async_computation.7 | async-start | bytes 1572864 | tf_op jit(solution)/shard_map/reduce_scatter | solution.py:56
  196.8 102.4 %all-reduce.15.cloned.1.call-start = ((), (), s32[]{:S(2)}) async-start(), calls=%async_computation.11 | async-start | bytes 2097152 | tf_op jit(solution)/shard_map/psum | solution.py:46
  236.9 9.6 copy-start
  250.2 49.0 %copy-start.8 = (f32[1024]{0:T(1024)S(1)}, f32[1024]{0:T(1024)}, u32[]{:S(2)}) copy-start(f32[1024]{0:T(1024)} %param.9) | copy-start | bytes 12292
  260.0 115.4 %all-reduce.11.cloned.1.call-start = ((), (), s32[]{:S(2)}) async-start(), calls=%async_computation.9 | async-start | bytes 4194304 | tf_op jit(solution)/shard_map/psum | solution.py:76
  311.8 145.4 %all-reduce.13.cloned.1.call-start = ((), (), s32[]{:S(2)}) async-start(), calls=%async_computation.10 | async-start | bytes 4194304 | tf_op jit(solution)/shard_map/psum | solution.py:79
  390.1 1.6 copy-start.4
  390.1 215.0 %all-gather.11.cloned.1.call-start = ((), (), s32[]{:S(2)}) async-start(), calls=%async_computation.6 | async-start | bytes 10485760 | tf_op jit(solution)/shard_map/all_gather | solution.py:66
  394.8 1.0 copy-start.6
  394.8 342.1 %all-gather.9.cloned.1.call-start = ((), (), s32[]{:S(2)}) async-start(), calls=%async_computation.5 | async-start | bytes 2621440 | tf_op jit(solution)/shard_map/all_gather | solution.py:65
  403.9 727.5 %all-reduce.9.cloned.1.call-start = ((), (), s32[]{:S(2)}) async-start(), calls=%async_computation.8 | async-start | bytes 33554432 | tf_op jit(solution)/shard_map/psum | solution.py:73
  412.6 1.0 copy-start.5
  440.4 16.8 %copy-start.2 = (bf16[128,64,128]{2,1,0:T(8,128)(2,1)S(1)}, bf16[128,64,128]{2,1,0:T(8,128)(2,1)}, u32[]{:S(2)}) copy-start(bf16[128,64,128]{2,1,0:T(8,128)(2,1)} %param.6) | copy-start | bytes 6291460
Sparse Core Ops, SparseCore 0:
  10.4 77.7 all-gather.6
  90.3 58.7 all-gather.4
  173.9 62.9 all-reduce.6
  239.6 20.3 reduce-scatter.1
  262.8 36.3 all-reduce.14
  311.9 63.4 all-reduce.10
  390.2 50.8 all-reduce.12
  444.3 687.0 all-reduce.8
Sparse Core Ops, SparseCore 1:
  394.9 210.2 all-gather.10
  606.6 130.3 all-gather.8
where the time goes:
time: 1160 us; the launch traced here: 1150 us
  waiting for transfers between devices  846 us (73%)
  blocking collectives  124 us (11%)
  matrix products  109 us (9%)
  local copies, waits for them, and re-layouts  46 us (4%)
  between operations  15.9 us (1%)
    psum x1, waiting for transfers between devices, local(): lax.psum((contract_first(activated, d_pre_b), jnp.sum(d_preact, axis=0)),...  380 us
    all_gather x1, waiting for transfers between devices, local(): lax.all_gather(hidden_all, 'batch', axis=0, tiled=True)  132 us
    all_gather x1, waiting for transfers between devices, local(): lax.all_gather(cot_rows, 'batch', axis=0, tiled=True)  105 us
    psum x1, waiting for transfers between devices, local(): lax.psum(contract_last(d_pre_b, w_in), 'col')  63.5 us
    all_gather x1, waiting for transfers between devices, local(): column_rows = lax.all_gather(regrouped, 'row', axis=2, tiled=True)  60.9 us
    all_to_all x1, blocking collectives, local(): lax.all_to_all(embeddings, 'col', split_axis=2, concat_axis=1, tiled=True)  49.2 us
    psum x1, blocking collectives, local(): lax.psum(jnp.einsum('bde,bdk->ek', emb_float, back_fold, precision=highes...  40.4 us
    psum x1, waiting for transfers between devices, local(): interact = lax.psum(partial_value, 'col')  40.1 us
  transfers between devices with their start and end apart: 10, of which 9 were waited for; matrix products, arithmetic and copies ran while one was open for 9% of the time, Pallas kernels for 0%

commit v1 on v0

--- a/solution.py
+++ b/solution.py
@@ -73,7 +73,9 @@
     grad_in, grad_bias = lax.psum(
         (contract_first(activated, d_pre_b), jnp.sum(d_preact, axis=0)), "batch"
     )
-    d_act = lax.psum(contract_last(d_pre_b, w_in), "col").reshape(tok_rows, emb_local, rank_cols)
+    d_act = jnp.sum(lax.all_gather(contract_last(d_pre_b, w_in), "col"), axis=0).reshape(
+        tok_rows, emb_local, rank_cols
+    )
     inner_term = lax.psum(jnp.sum(d_act * normed, axis=(1, 2)), "row") / feature_count
     d_inter = (inv_rms * (d_act - normed * inner_term[:, None, None])).astype(jnp.bfloat16)
     back_fold = lax.psum(

time: 1160 us -> 1210 us (1.043)
  waiting for transfers between devices: 846 us -> 890 us
    psum x1, waiting for transfers between devices: 380 us -> 523 us  [local(): lax.psum((contract_first(activated, d_pre_b), jnp.sum(d_preact, axis=0)),...]
    all_gather x1, waiting for transfers between devices: 132 us -> 45.5 us  [local(): lax.all_gather(hidden_all, 'batch', axis=0, tiled=True)]
    psum x1 -> x0, waiting for transfers between devices: 63.5 us -> none  [local(): lax.psum(contract_last(d_pre_b, w_in), 'col')]
    all_gather x0 -> x1, waiting for transfers between devices: none -> 41.2 us  [local(): lax.all_gather(contract_last(d_pre_b, w_in), 'col')]
    psum x1, waiting for transfers between devices: 0.01 us -> 38.4 us  [local(): lax.psum(jnp.einsum('bek,bde->bdk', d_inter, embeddings, preferred_elemen...]
    all_gather x1, waiting for transfers between devices: 105 us -> 75.4 us  [local(): lax.all_gather(cot_rows, 'batch', axis=0, tiled=True)]
    unnamed x23 -> x19, local copies, waits for them, and re-layouts: 35.4 us -> 32.8 us
  transfers between devices with their start and end apart: 10 -> 10, of which waited for: 9 -> 10; matrix products, arithmetic and copies ran while one was open for 9% -> 10% of each run, Pallas kernels for 0% -> 0%
where the time goes in v1:
time: 1210 us; the launch traced here: 1200 us
  waiting for transfers between devices  890 us (74%)
  blocking collectives  130 us (11%)
  matrix products  108 us (9%)
  local copies, waits for them, and re-layouts  46.3 us (4%)
  between operations  14.5 us (1%)
  other arithmetic  14 us (1%)
    psum x1, waiting for transfers between devices, local(): lax.psum((contract_first(activated, d_pre_b), jnp.sum(d_preact, axis=0)),...  523 us
    all_gather x1, waiting for transfers between devices, local(): lax.all_gather(cot_rows, 'batch', axis=0, tiled=True)  75.4 us
    all_gather x1, waiting for transfers between devices, local(): column_rows = lax.all_gather(regrouped, 'row', axis=2, tiled=True)  60.9 us
    all_to_all x1, blocking collectives, local(): lax.all_to_all(embeddings, 'col', split_axis=2, concat_axis=1, tiled=True)  49.2 us
    all_gather x1, waiting for transfers between devices, local(): lax.all_gather(hidden_all, 'batch', axis=0, tiled=True)  45.5 us
    all_gather x1, waiting for transfers between devices, local(): lax.all_gather(contract_last(d_pre_b, w_in), 'col')  41.2 us
    psum x1, waiting for transfers between devices, local(): interact = lax.psum(partial_value, 'col')  40.1 us
    psum x1, blocking collectives, local(): lax.psum(jnp.einsum('bde,bdk->ek', emb_float, back_fold, precision=highes...  39.7 us
  transfers between devices with their start and end apart: 10, of which 10 were waited for; matrix products, arithmetic and copies ran while one was open for 10% of the time, Pallas kernels for 0%

profile of v1, /device:TPU:0, one launch (start us, length us, event | category | flops | bytes accessed | tf_op | source)
XLA Modules:
  0.0 1202.7 jit_solution(12258625688629483250)
XLA Ops:
  12.0 49.2 %all_to_all.18 = bf16[128,64,128]{0,1,2:T(8,128)(2,1)S(1)} all-to-all(bf16[128,64,128]{0,1,2:T(8,128)(2,1)} %copy.22), channel_id=1, replica_groups=mesh['batch'=4,'row'=4,'col'=2] {'col'}, dimensions={2} | all-to-all | bytes 4194304 | tf_op jit(solution)/shard_map/all_to_all | solution.py:30
  66.9 20.5 %all-gather.9.cloned.1.call-done = bf16[128,128,128]{2,1,0:T(8,128)(2,1)} async-done(((bf16[128,64,128]{2,1,0:T(8,128)(2,1)}), bf16[128,128,128]{2,1,0:T(8,128)(2,1)}) %all-gather.9.cloned.1.call-update) | async-done | bytes 4194320 | tf_op jit(solution)/shard_map/all_gather | solution.py:29
  87.3 60.9 %all-gather.7.cloned.1.call-done = bf16[128,128,256]{1,2,0:T(8,128)(2,1)} async-done(((bf16[128,128,64]{1,2,0:T(8,128)(2,1)}), bf16[128,128,256]{1,2,0:T(8,128)(2,1)}) %all-gather.7.cloned.1.call-update) | async-done | bytes 8388624 | tf_op jit(solution)/shard_map/all_gather | solution.py:31
  148.3 13.1 %fusion.24 = f32[128,256,128]{2,1,0:T(8,128)} fusion(bf16[128,128,256]{1,2,0:T(8,128)(2,1)} %all-gather.7.cloned.1.call-done, bf16[128,128,128]{2,1,0:T(8,128)(2,1)} %all-gather.9.cloned.1.call-done), kind=kOutput, calls=%fused_computation.32 | convolution fusion | flops 1073741824 | bytes 29360128 | tf_op jit(solution)/shard_map/bdj,bde->bje/dot_general | solution.py:32
  161.3 11.5 fusion.25
  174.5 21.4 %fusion.8 = f32[128,2048]{1,0:T(8,128)} fusion(bf16[2048,64,128]{2,1,0:T(8,128)(2,1)} %param.10, bf16[128,64,128]{2,1,0:T(8,128)(2,1)S(1)} %copy-done.3), kind=kOutput, calls=%fused_computation.7 | convolution fusion | flops 4294967296 | bytes 36700160 | tf_op jit(solution)/shard_map/dot_general | solution.py:16
  196.0 40.1 %all-reduce.6.cloned.1.call-done = f32[128,128,32]{1,2,0:T(8,128)} async-done(((f32[128,128,32]{1,2,0:T(8,128)}), f32[128,128,32]{1,2,0:T(8,128)}) %all-reduce.6.cloned.1.call-update) | async-done | bytes 2097168 | tf_op jit(solution)/shard_map/psum | solution.py:40
  238.8 6.8 psum.64
  259.2 39.2 %all-reduce.12.cloned.1.call-done = (f32[128,1024]{1,0:T(8,128)}, f32[128,1024]{1,0:T(8,128)}) async-done(((f32[128,1024]{1,0:T(8,128)}, f32[128,1024]{1,0:T(8,128)}), (f32[128,1024]{1,0:T(8,128)}, f32[128,1024]{1,0:T(8,128)})) %all-reduce.12.cloned.1.call-update) | async-done | bytes 1048592 | tf_op jit(solution)/shard_map/psum | solution.py:46
  300.5 7.6 fusion.18
  312.9 13.6 %all_gather.23 = bf16[128,2048]{1,0:T(8,128)(2,1)} all-gather(bf16[128,1024]{1,0:T(8,128)(2,1)} %get-tuple-element.9), channel_id=1, replica_groups=mesh['batch'=4,'row'=4,'col'=2] {'col'}, dimensions={1}, use_global_device_ids=true | all-gather | bytes 786432 | tf_op jit(solution)/shard_map/all_gather | solution.py:48
  326.6 41.2 %all-gather.15.cloned.1.call-done = f32[256,4096]{1,0:T(8,128)} async-done(((f32[128,4096]{1,0:T(8,128)}), f32[256,4096]{1,0:T(8,128)}) %all-gather.15.cloned.1.call-update) | async-done | bytes 4194320 | tf_op jit(solution)/shard_map/all_gather | solution.py:76
  381.9 7.0 psum.69
  394.0 8.5 fusion.20
  403.5 25.7 %fusion.12 = bf16[16,8,64,128]{3,1,2,0:T(8,128)(2,1)S(1)} fusion(bf16[128,2048]{1,0:T(8,128)(2,1)S(1)} %copy-done.4, bf16[256,8,64,128]{3,2,1,0:T(8,128)(2,1)} %bitcast.62), kind=kOutput, calls=%fused_computation.14 | convolution fusion | flops 4296015872 | bytes 36175872 | tf_op jit(solution)/shard_map/dot_general | solution.py:51
  431.2 13.2 %psum.68 = f32[1024]{0:T(1024)} all-reduce(f32[1024]{0:T(1024)S(1)} %get-tuple-element.7), channel_id=1, replica_groups=mesh['batch'=4,'row'=4,'col'=2] {'batch'}, use_global_device_ids=true, to_apply=%region_8.9 | all-reduce | flops 1024 | bytes 8192 | tf_op jit(solution)/shard_map/psum | solution.py:73
  444.4 75.4 %all-gather.13.cloned.1.call-done = bf16[512,8192]{1,0:T(8,128)(2,1)} async-done(((bf16[128,8192]{1,0:T(8,128)(2,1)}), bf16[512,8192]{1,0:T(8,128)(2,1)}) %all-gather.13.cloned.1.call-update) | async-done | bytes 8388624 | tf_op jit(solution)/shard_map/all_gather | solution.py:66
  519.8 45.5 %all-gather.11.cloned.1.call-done = bf16[512,2048]{1,0:T(8,128)(2,1)} async-done(((bf16[128,2048]{1,0:T(8,128)(2,1)}), bf16[512,2048]{1,0:T(8,128)(2,1)}) %all-gather.11.cloned.1.call-update) | async-done | bytes 2097168 | tf_op jit(solution)/shard_map/all_gather | solution.py:65
  565.3 7.2 convolution_bitcast_fusion
  572.6 6.9 copy.40
  579.5 38.4 %all-reduce.10.cloned.1.call-done = f32[128,64,32]{1,2,0:T(8,128)} async-done(((f32[128,64,32]{1,2,0:T(8,128)}), f32[128,64,32]{1,2,0:T(8,128)}) %all-reduce.10.cloned.1.call-update) | async-done | bytes 1048592 | tf_op jit(solution)/shard_map/psum | solution.py:81
  620.6 39.7 %psum.71 = f32[128,32]{0,1:T(8,128)} all-reduce(f32[128,32]{0,1:T(8,128)S(1)} %convolution_bitcast_fusion.2), channel_id=1, replica_groups=mesh['batch'=4,'row'=4,'col'=2] {'batch','col'}, use_global_device_ids=true, to_apply=%region_13.14 | all-reduce | flops 4096 | bytes 32768 | tf_op jit(solution)/shard_map/psum | solution.py:84
  660.3 523.4 %all-reduce.8.cloned.1.call-done = f32[4096,1024]{1,0:T(8,128)} async-done(((f32[4096,1024]{1,0:T(8,128)}), f32[4096,1024]{1,0:T(8,128)}) %all-reduce.8.cloned.1.call-update) | async-done | bytes 16777232 | tf_op jit(solution)/shard_map/psum | solution.py:73
  1183.7 12.0 copy.62
  (56 shorter events, 60.1 us)
Async XLA Ops:
  7.2 1.6 copy-start.1
  7.2 80.2 %all-gather.9.cloned.1.call-start = ((), (), s32[]{:S(2)}) async-start(), calls=%async_computation.3 | async-start | bytes 6291456 | tf_op jit(solution)/shard_map/all_gather | solution.py:29
  7.9 140.4 %all-gather.7.cloned.1.call-start = ((), (), s32[]{:S(2)}) async-start(), calls=%async_computation.2 | async-start | bytes 10485760 | tf_op jit(solution)/shard_map/all_gather | solution.py:31
  65.9 0.8 copy-start.5
  65.9 170.1 %all-reduce.6.cloned.1.call-start = ((), (), s32[]{:S(2)}) async-start(), calls=%async_computation.4 | async-start | bytes 4194304 | tf_op jit(solution)/shard_map/psum | solution.py:40
  172.9 1.6 copy-start.3
  172.9 86.2 %reduce-scatter.2.cloned.1.call-start = ((), (), s32[]{:S(2)}) async-start(), calls=%async_computation.7 | async-start | bytes 1572864 | tf_op jit(solution)/shard_map/reduce_scatter | solution.py:56
  195.9 102.4 %all-reduce.12.cloned.1.call-start = ((), (), s32[]{:S(2)}) async-start(), calls=%async_computation.11 | async-start | bytes 2097152 | tf_op jit(solution)/shard_map/psum | solution.py:46
  236.1 9.6 copy-start
  249.4 49.0 %copy-start.6 = (f32[1024]{0:T(1024)S(1)}, f32[1024]{0:T(1024)}, u32[]{:S(2)}) copy-start(f32[1024]{0:T(1024)} %param.9) | copy-start | bytes 12292
  259.2 108.7 %all-gather.15.cloned.1.call-start = ((), (), s32[]{:S(2)}) async-start(), calls=%async_computation.10 | async-start | bytes 6291456 | tf_op jit(solution)/shard_map/all_gather | solution.py:76
  308.1 211.7 %all-gather.13.cloned.1.call-start = ((), (), s32[]{:S(2)}) async-start(), calls=%async_computation.6 | async-start | bytes 10485760 | tf_op jit(solution)/shard_map/all_gather | solution.py:66
  312.9 252.4 %all-gather.11.cloned.1.call-start = ((), (), s32[]{:S(2)}) async-start(), calls=%async_computation.5 | async-start | bytes 2621440 | tf_op jit(solution)/shard_map/all_gather | solution.py:65
  326.6 291.3 %all-reduce.10.cloned.1.call-start = ((), (), s32[]{:S(2)}) async-start(), calls=%async_computation.9 | async-start | bytes 4194304 | tf_op jit(solution)/shard_map/psum | solution.py:81
  393.8 789.9 %all-reduce.8.cloned.1.call-start = ((), (), s32[]{:S(2)}) async-start(), calls=%async_computation.8 | async-start | bytes 33554432 | tf_op jit(solution)/shard_map/psum | solution.py:73
  402.5 1.0 copy-start.4
  572.5 45.3 %copy-start.2 = (bf16[128,64,128]{2,1,0:T(8,128)(2,1)S(1)}, bf16[128,64,128]{2,1,0:T(8,128)(2,1)}, u32[]{:S(2)}) copy-start(bf16[128,64,128]{2,1,0:T(8,128)(2,1)} %param.6) | copy-start | bytes 6291460
Sparse Core Ops, SparseCore 0:
  9.5 77.7 all-gather.8
  89.5 58.7 all-gather.6
  173.0 62.9 all-reduce.5
  238.7 20.3 reduce-scatter.1
  262.0 36.3 all-reduce.11
  308.2 59.5 all-gather.14
  370.0 149.7 all-gather.12
  521.4 43.8 all-gather.10
  567.7 50.1 all-reduce.9
  620.8 562.8 all-reduce.7
